TPU v7x, 32 devices: a whole 2x2x4 slice. The times are simulated.
32 devices in a mesh: zero: 16 (over z, y, core), width: 2 (over x).
Axes of the slice: x: 2, y: 2, z: 4, core: 2. Of those that a mesh axis runs over, the one named last changes fastest.
Arguments:
- slopes_in: float32 [128, 128, 4096], P(None, 'zero', 'width'), may hold values from -6 to 6
- moments_in: float32 [128, 128, 4096], P(None, 'zero', 'width'), may hold values from -6 to 6
- weights_in: float32 [128, 128, 4096], P(None, 'zero', 'width'), may hold values from -0.1875 to 0.1875
Outputs:
- new_weights: float32 [128, 128, 4096], P(None, 'zero', 'width')
- new_momentum: float32 [128, 128, 4096], P(None, 'zero', 'width')
All inputs are finite; a program needn't handle non-finite values.
Results may differ from a plain program's by a relative error of at most 0.0001.
Values sent between devices are 32-bit elements; how exact they have to be, the bound alone decides.
A program may use at most 128 MiB of HBM per device.

v0:
```python
import jax
import jax.numpy as jnp
from jax import lax
from jax.sharding import PartitionSpec as P

ITERS = 3
hold_rate = 0.8
learn_rate = 0.8
decay_rate = 0.1


def body(slopes_in, moments_in, weights_in):
    new_momentum = hold_rate * moments_in + slopes_in
    direction = hold_rate * new_momentum + slopes_in
    moved = lax.all_to_all(direction, "zero", split_axis=0, concat_axis=1, tiled=True)
    total = lax.psum(jnp.sum(moved * moved, axis=(1, 2), keepdims=True), "width")
    iterate = moved * lax.rsqrt(total + 1e-06)
    for step in range(ITERS):
        gram = lax.psum(
            jnp.einsum("mik,mjk->mij", iterate, iterate, precision=lax.Precision.HIGHEST), "width"
        )
        mixed = -4.775 * gram + 2.0315 * jnp.einsum(
            "mij,mjk->mik", gram, gram, precision=lax.Precision.HIGHEST
        )
        iterate = 3.4445 * iterate + jnp.einsum(
            "mij,mjk->mik", mixed, iterate, precision=lax.Precision.HIGHEST
        )
    back = lax.all_to_all(iterate, "zero", split_axis=1, concat_axis=0, tiled=True)
    new_weights = (1.0 - learn_rate * decay_rate) * weights_in - learn_rate * back
    return (new_weights, new_momentum)


def solution(mesh):
    in_specs = (P(None, "zero", "width"), P(None, "zero", "width"), P(None, "zero", "width"))
    out_specs = (P(None, "zero", "width"), P(None, "zero", "width"))
    return jax.shard_map(body, mesh=mesh, in_specs=in_specs, out_specs=out_specs, check_vma=False)
```

profile of v0, /device:TPU:1, one launch (start us, length us, event | category | flops | bytes accessed | tf_op | source)
XLA Modules:
  0.0 609.2 jit_solution(12829300528116619400)
XLA Ops:
  7.2 0.0 all-reduce.4.cloned.1.call-start
  7.2 9.3 %multiply_add_fusion.3 = (f32[128,8,2048]{2,1,0:T(8,128)S(1)}, f32[128,8,2048]{2,1,0:T(8,128)}) fusion(f32[128,8,2048]{2,1,0:T(8,128)} %param.3, f32[128,8,2048]{2,1,0:T(8,128)} %param.4), kind=kLoop, calls=%fused_computation.7 | loop fusion | flops 8388608 | bytes 33554432 | tf_op jit(solution)/shard_map/add | solution.py:14
  16.5 189.7 %all_to_all.27 = f32[128,8,2048]{2,1,0:T(8,128)S(1)} all-to-all(f32[128,8,2048]{2,1,0:T(8,128)S(1)} %get-tuple-element.2), channel_id=1, replica_groups=mesh['zero'=16,'width'=2] {'zero'}, dimensions={0} | all-to-all | bytes 16777216 | tf_op jit(solution)/shard_map/all_to_all | solution.py:15
  206.2 0.0 copy-start
  206.2 3.4 copy-done
  209.5 0.8 fusion
  210.3 4.1 psum.28
  214.4 12.9 %fusion.2 = f32[8,128,128]{2,1,0:T(8,128)} fusion(f32[16,8,8,2048]{3,2,1,0:T(8,128)} %bitcast.38, f32[8]{0:T(128)S(1)} %rsqrt_bitcast_fusion), kind=kOutput, calls=%fused_computation.10 | convolution fusion | flops 3223322624 | bytes 8912928 | tf_op jit(solution)/shard_map/mik,mjk->mij/dot_general | solution.py:20
  227.3 0.0 all-reduce.4.cloned.1.call-update
  227.3 0.0 all-reduce.6.cloned.1.call-start
  227.4 29.3 %all-reduce.4.cloned.1.call-done = f32[8,128,128]{2,1,0:T(8,128)} async-done(((f32[8,128,128]{2,1,0:T(8,128)}), f32[8,128,128]{2,1,0:T(8,128)}) %all-reduce.4.cloned.1.call-update) | async-done | bytes 524304 | tf_op jit(solution)/shard_map/psum | solution.py:19
  256.7 2.1 fusion.7
  258.8 11.7 %multiply_add_fusion.2 = f32[8,128,2048]{2,1,0:T(8,128)S(1)} fusion(f32[16,8,8,2048]{3,2,1,0:T(8,128)} %bitcast.39, f32[8,128,128]{2,1,0:T(8,128)S(1)} %fusion.7, f32[8]{0:T(128)S(1)} %rsqrt_bitcast_fusion), kind=kOutput, calls=%fused_computation.6 | convolution fusion | flops 3229614080 | bytes 17301536 | tf_op jit(solution)/shard_map/mij,mjk->mik/dot_general | solution.py:25
  270.5 0.0 copy-start.1
  270.5 3.4 copy-done.1
  273.9 8.5 %fusion.8 = f32[8,128,128]{2,1,0:T(8,128)} fusion(f32[8,128,2048]{2,1,0:T(8,128)S(1)} %multiply_add_fusion.2), kind=kOutput, calls=%fused_computation.21 | convolution fusion | flops 3221225472 | bytes 8912896 | tf_op jit(solution)/shard_map/mik,mjk->mij/dot_general | solution.py:20
  282.4 0.0 all-reduce.6.cloned.1.call-update
  282.4 0.0 all-reduce.8.cloned.1.call-start
  282.5 28.8 %all-reduce.6.cloned.1.call-done = f32[8,128,128]{2,1,0:T(8,128)} async-done(((f32[8,128,128]{2,1,0:T(8,128)}), f32[8,128,128]{2,1,0:T(8,128)}) %all-reduce.6.cloned.1.call-update) | async-done | bytes 524304 | tf_op jit(solution)/shard_map/psum | solution.py:19
  311.2 2.1 fusion.6
  313.3 14.1 %multiply_add_fusion.1 = f32[8,128,2048]{2,1,0:T(8,128)S(1)} fusion(f32[8,128,2048]{2,1,0:T(8,128)} %copy-done.1, f32[8,128,128]{2,1,0:T(8,128)S(1)} %fusion.6), kind=kOutput, calls=%fused_computation.5 | convolution fusion | flops 3225419776 | bytes 17301504 | tf_op jit(solution)/shard_map/mij,mjk->mik/dot_general | solution.py:25
  327.4 0.0 copy-start.2
  327.4 3.4 copy-done.2
  330.8 8.5 %fusion.9 = f32[8,128,128]{2,1,0:T(8,128)} fusion(f32[8,128,2048]{2,1,0:T(8,128)S(1)} %multiply_add_fusion.1), kind=kOutput, calls=%fused_computation.22 | convolution fusion | flops 3221225472 | bytes 8912896 | tf_op jit(solution)/shard_map/mik,mjk->mij/dot_general | solution.py:20
  339.3 0.0 all-reduce.8.cloned.1.call-update
  339.4 28.8 %all-reduce.8.cloned.1.call-done = f32[8,128,128]{2,1,0:T(8,128)} async-done(((f32[8,128,128]{2,1,0:T(8,128)}), f32[8,128,128]{2,1,0:T(8,128)}) %all-reduce.8.cloned.1.call-update) | async-done | bytes 524304 | tf_op jit(solution)/shard_map/psum | solution.py:19
  368.1 2.1 fusion.5
  370.2 15.0 %multiply_add_fusion = f32[8,128,2048]{2,1,0:T(8,128)S(1)} fusion(f32[8,128,2048]{2,1,0:T(8,128)} %copy-done.2, f32[8,128,128]{2,1,0:T(8,128)S(1)} %fusion.5), kind=kOutput, calls=%fused_computation.4 | convolution fusion | flops 3225419776 | bytes 17301504 | tf_op jit(solution)/shard_map/mij,mjk->mik/dot_general | solution.py:25
  385.2 4.9 copy.8
  390.1 188.9 %all_to_all.28 = f32[8,128,2048]{2,0,1:T(8,128)S(1)} all-to-all(f32[8,128,2048]{2,0,1:T(8,128)S(1)} %copy.8), channel_id=1, replica_groups=mesh['zero'=16,'width'=2] {'zero'}, dimensions={1} | all-to-all | bytes 16777216 | tf_op jit(solution)/shard_map/all_to_all | solution.py:28
  579.0 1.8 broadcast_multiply_fusion
  580.8 9.7 %copy.9 = f32[16,8,8,2048]{3,2,1,0:T(8,128)} copy(f32[16,8,8,2048]{3,1,2,0:T(8,128)S(1)} %bitcast.40) | data formatting | bytes 16777216 | tf_op jit(solution)/shard_map/mul | solution.py:29
  590.5 12.0 %bitcast_subtract_fusion = f32[128,8,2048]{2,1,0:T(8,128)} fusion(f32[16,8,8,2048]{3,2,1,0:T(8,128)} %copy.9, f32[128,8,2048]{2,1,0:T(8,128)} %param.5), kind=kLoop, calls=%fused_computation.1 | loop fusion | flops 4194304 | bytes 25165824 | tf_op jit(solution)/shard_map/sub | solution.py:29
  (1 shorter events, 0.0 us)
Async XLA Ops:
  7.2 249.5 %all-reduce.4.cloned.1.call-start = ((), (), s32[]{:S(2)}) async-start(), calls=%async_computation.2 | async-start | bytes 1048576 | tf_op jit(solution)/shard_map/psum | solution.py:19
  206.2 3.4 copy-start
  227.3 83.9 %all-reduce.6.cloned.1.call-start = ((), (), s32[]{:S(2)}) async-start(), calls=%async_computation.3 | async-start | bytes 1048576 | tf_op jit(solution)/shard_map/psum | solution.py:19
  270.5 3.4 copy-start.1
  282.4 85.7 %all-reduce.8.cloned.1.call-start = ((), (), s32[]{:S(2)}) async-start(), calls=%async_computation.4 | async-start | bytes 1048576 | tf_op jit(solution)/shard_map/psum | solution.py:19
  327.4 3.4 copy-start.2
Sparse Core Ops, SparseCore 0:
  227.5 29.1 all-reduce.3
  282.5 28.6 all-reduce.5
  339.5 28.6 all-reduce.7
where the time goes:
time: 618 us; the launch traced here: 609 us
  blocking collectives  383 us (62%)
  waiting for transfers between devices  86.9 us (14%)
  matrix products  76.9 us (12%)
  local copies, waits for them, and re-layouts  24.7 us (4%)
  other arithmetic  23.9 us (4%)
  between operations  14 us (2%)
    all_to_all x1, blocking collectives, body(): lax.all_to_all(direction, 'zero', split_axis=0, concat_axis=1, tiled=True)  190 us
    all_to_all x1, blocking collectives, body(): lax.all_to_all(iterate, 'zero', split_axis=1, concat_axis=0, tiled=True)  189 us
    psum x3, waiting for transfers between devices, body(): lax.psum(jnp.einsum('mik,mjk->mij', iterate, iterate, precision=lax.Preci...  86.9 us
    dot_general x3, matrix products, body(): jnp.einsum('mij,mjk->mik', mixed, iterate, precision=lax.Precision.HIGHEST)  40.8 us
    dot_general x3, matrix products, body(): jnp.einsum('mik,mjk->mij', iterate, iterate, precision=lax.Precision.HIGH...  29.9 us
  transfers between devices with their start and end apart: 3, of which 3 were waited for; matrix products, arithmetic and copies ran while one was open for 0% of the time, Pallas kernels for 0%

commit v1 on v0

--- a/solution.py
+++ b/solution.py
@@ -2,6 +2,7 @@
 import jax.numpy as jnp
 from jax import lax
 from jax.sharding import PartitionSpec as P
+from jax.lax import all_gather
 
 ITERS = 3
 hold_rate = 0.8
@@ -16,7 +17,13 @@
     total = lax.psum(jnp.sum(moved * moved, axis=(1, 2), keepdims=True), "width")
     iterate = moved * lax.rsqrt(total + 1e-06)
     for step in range(ITERS):
-        gram = lax.psum(
+
+        def pair_tasks(incoming_x, lane_axis):
+            view_out = all_gather(incoming_x, lane_axis)
+            z_new = jnp.sum(view_out, 0)
+            return z_new
+
+        gram = pair_tasks(
             jnp.einsum("mik,mjk->mij", iterate, iterate, precision=lax.Precision.HIGHEST), "width"
         )
         mixed = -4.775 * gram + 2.0315 * jnp.einsum(

time: 618 us -> 595 us (0.963)
  waiting for transfers between devices: 86.9 us -> 64.8 us
    psum x3 -> x0, waiting for transfers between devices: 86.9 us -> none  [body(): lax.psum(jnp.einsum('mik,mjk->mij', iterate, iterate, precision=lax.Preci...]
    all_gather x0 -> x3, waiting for transfers between devices: none -> 64.8 us  [pair_tasks(): view_out = all_gather(incoming_x, lane_axis)]
where the time goes in v1:
time: 595 us; the launch traced here: 587 us
  blocking collectives  383 us (64%)
  matrix products  72.7 us (12%)
  waiting for transfers between devices  64.8 us (11%)
  other arithmetic  27.9 us (5%)
  local copies, waits for them, and re-layouts  24.7 us (4%)
  between operations  14 us (2%)
    all_to_all x1, blocking collectives, body(): lax.all_to_all(direction, 'zero', split_axis=0, concat_axis=1, tiled=True)  190 us
    all_to_all x1, blocking collectives, body(): lax.all_to_all(iterate, 'zero', split_axis=1, concat_axis=0, tiled=True)  189 us
    all_gather x3, waiting for transfers between devices, pair_tasks(): view_out = all_gather(incoming_x, lane_axis)  64.8 us
    dot_general x3, matrix products, body(): jnp.einsum('mij,mjk->mik', mixed, iterate, precision=lax.Precision.HIGHEST)  40.8 us
    dot_general x3, matrix products, body(): jnp.einsum('mik,mjk->mij', iterate, iterate, precision=lax.Precision.HIGH...  30 us
    sub x1, other arithmetic, body(): (1.0 - learn_rate * decay_rate) * weights_in - learn_rate * back  12 us
  transfers between devices with their start and end apart: 3, of which 3 were waited for; matrix products, arithmetic and copies ran while one was open for 0% of the time, Pallas kernels for 0%

profile of v1, /device:TPU:1, one launch (start us, length us, event | category | flops | bytes accessed | tf_op | source)
XLA Modules:
  0.0 587.0 jit_solution(14829581679985808944)
XLA Ops:
  7.2 0.0 all-gather.7.cloned.1.call-start
  7.2 9.3 %multiply_add_fusion.3 = (f32[128,8,2048]{2,1,0:T(8,128)S(1)}, f32[128,8,2048]{2,1,0:T(8,128)}) fusion(f32[128,8,2048]{2,1,0:T(8,128)} %param.3, f32[128,8,2048]{2,1,0:T(8,128)} %param.4), kind=kLoop, calls=%fused_computation.7 | loop fusion | flops 8388608 | bytes 33554432 | tf_op jit(solution)/shard_map/add | solution.py:15
  16.5 189.7 %all_to_all.27 = f32[128,8,2048]{2,1,0:T(8,128)S(1)} all-to-all(f32[128,8,2048]{2,1,0:T(8,128)S(1)} %get-tuple-element.2), channel_id=1, replica_groups=mesh['zero'=16,'width'=2] {'zero'}, dimensions={0} | all-to-all | bytes 16777216 | tf_op jit(solution)/shard_map/all_to_all | solution.py:16
  206.2 0.0 copy-start
  206.2 3.4 copy-done
  209.5 0.8 fusion
  210.3 4.1 psum.7
  214.4 12.9 %fusion.2 = f32[8,128,128]{2,1,0:T(8,128)} fusion(f32[16,8,8,2048]{3,2,1,0:T(8,128)} %bitcast.41, f32[8]{0:T(128)S(1)} %rsqrt_bitcast_fusion), kind=kOutput, calls=%fused_computation.10 | convolution fusion | flops 3223322624 | bytes 8912928 | tf_op jit(solution)/shard_map/mik,mjk->mij/dot_general | solution.py:27
  227.3 0.0 all-gather.7.cloned.1.call-update
  227.3 0.0 all-gather.9.cloned.1.call-start
  227.4 21.9 %all-gather.7.cloned.1.call-done = f32[16,128,128]{2,1,0:T(8,128)} async-done(((f32[8,128,128]{2,1,0:T(8,128)}), f32[16,128,128]{2,1,0:T(8,128)}) %all-gather.7.cloned.1.call-update) | async-done | bytes 1048592 | tf_op jit(solution)/shard_map/all_gather | solution.py:22
  249.3 1.3 reduce_sum.37
  250.7 0.7 fusion.7
  251.4 11.7 %multiply_add_fusion.2 = f32[8,128,2048]{2,1,0:T(8,128)S(1)} fusion(f32[16,8,8,2048]{3,2,1,0:T(8,128)} %bitcast.42, f32[8,128,128]{2,1,0:T(8,128)S(1)} %fusion.7, f32[8]{0:T(128)S(1)} %rsqrt_bitcast_fusion), kind=kOutput, calls=%fused_computation.6 | convolution fusion | flops 3229614080 | bytes 17301536 | tf_op jit(solution)/shard_map/mij,mjk->mik/dot_general | solution.py:32
  263.0 0.0 copy-start.1
  263.0 3.4 copy-done.1
  266.4 8.5 %fusion.8 = f32[8,128,128]{2,1,0:T(8,128)} fusion(f32[8,128,2048]{2,1,0:T(8,128)S(1)} %multiply_add_fusion.2), kind=kOutput, calls=%fused_computation.21 | convolution fusion | flops 3221225472 | bytes 8912896 | tf_op jit(solution)/shard_map/mik,mjk->mij/dot_general | solution.py:27
  275.0 0.0 all-gather.9.cloned.1.call-update
  275.0 0.0 all-gather.11.cloned.1.call-start
  275.0 21.4 %all-gather.9.cloned.1.call-done = f32[16,128,128]{2,1,0:T(8,128)} async-done(((f32[8,128,128]{2,1,0:T(8,128)}), f32[16,128,128]{2,1,0:T(8,128)}) %all-gather.9.cloned.1.call-update) | async-done | bytes 1048592 | tf_op jit(solution)/shard_map/all_gather | solution.py:22
  296.4 1.3 reduce_sum.38
  297.8 0.7 fusion.6
  298.4 14.1 %multiply_add_fusion.1 = f32[8,128,2048]{2,1,0:T(8,128)S(1)} fusion(f32[8,128,2048]{2,1,0:T(8,128)} %copy-done.1, f32[8,128,128]{2,1,0:T(8,128)S(1)} %fusion.6), kind=kOutput, calls=%fused_computation.5 | convolution fusion | flops 3225419776 | bytes 17301504 | tf_op jit(solution)/shard_map/mij,mjk->mik/dot_general | solution.py:32
  312.5 0.0 copy-start.2
  312.6 3.4 copy-done.2
  315.9 8.5 %fusion.9 = f32[8,128,128]{2,1,0:T(8,128)} fusion(f32[8,128,2048]{2,1,0:T(8,128)S(1)} %multiply_add_fusion.1), kind=kOutput, calls=%fused_computation.22 | convolution fusion | flops 3221225472 | bytes 8912896 | tf_op jit(solution)/shard_map/mik,mjk->mij/dot_general | solution.py:27
  324.5 0.0 all-gather.11.cloned.1.call-update
  324.5 21.4 %all-gather.11.cloned.1.call-done = f32[16,128,128]{2,1,0:T(8,128)} async-done(((f32[8,128,128]{2,1,0:T(8,128)}), f32[16,128,128]{2,1,0:T(8,128)}) %all-gather.11.cloned.1.call-update) | async-done | bytes 1048592 | tf_op jit(solution)/shard_map/all_gather | solution.py:22
  345.9 1.3 reduce_sum.39
  347.3 0.7 fusion.5
  347.9 15.0 %multiply_add_fusion = f32[8,128,2048]{2,1,0:T(8,128)S(1)} fusion(f32[8,128,2048]{2,1,0:T(8,128)} %copy-done.2, f32[8,128,128]{2,1,0:T(8,128)S(1)} %fusion.5), kind=kOutput, calls=%fused_computation.4 | convolution fusion | flops 3225419776 | bytes 17301504 | tf_op jit(solution)/shard_map/mij,mjk->mik/dot_general | solution.py:32
  363.0 4.9 copy.8
  367.8 188.9 %all_to_all.28 = f32[8,128,2048]{2,0,1:T(8,128)S(1)} all-to-all(f32[8,128,2048]{2,0,1:T(8,128)S(1)} %copy.8), channel_id=1, replica_groups=mesh['zero'=16,'width'=2] {'zero'}, dimensions={1} | all-to-all | bytes 16777216 | tf_op jit(solution)/shard_map/all_to_all | solution.py:35
  556.7 1.8 broadcast_multiply_fusion
  558.5 9.7 %copy.9 = f32[16,8,8,2048]{3,2,1,0:T(8,128)} copy(f32[16,8,8,2048]{3,1,2,0:T(8,128)S(1)} %bitcast.43) | data formatting | bytes 16777216 | tf_op jit(solution)/shard_map/mul | solution.py:36
  568.3 12.0 %bitcast_subtract_fusion = f32[128,8,2048]{2,1,0:T(8,128)} fusion(f32[16,8,8,2048]{3,2,1,0:T(8,128)} %copy.9, f32[128,8,2048]{2,1,0:T(8,128)} %param.5), kind=kLoop, calls=%fused_computation.1 | loop fusion | flops 4194304 | bytes 25165824 | tf_op jit(solution)/shard_map/sub | solution.py:36
  (1 shorter events, 0.0 us)
Async XLA Ops:
  7.2 242.2 %all-gather.7.cloned.1.call-start = ((), (), s32[]{:S(2)}) async-start(), calls=%async_computation.2 | async-start | bytes 1572864 | tf_op jit(solution)/shard_map/all_gather | solution.py:22
  206.2 3.4 copy-start
  227.3 69.1 %all-gather.9.cloned.1.call-start = ((), (), s32[]{:S(2)}) async-start(), calls=%async_computation.3 | async-start | bytes 1572864 | tf_op jit(solution)/shard_map/all_gather | solution.py:22
  263.0 3.4 copy-start.1
  275.0 71.0 %all-gather.11.cloned.1.call-start = ((), (), s32[]{:S(2)}) async-start(), calls=%async_computation.4 | async-start | bytes 1572864 | tf_op jit(solution)/shard_map/all_gather | solution.py:22
  312.5 3.4 copy-start.2
Sparse Core Ops, SparseCore 0:
  227.5 21.8 all-gather.6
  275.1 21.2 all-gather.8
  324.6 21.2 all-gather.10
